TPU v7x, 256 devices: a whole 4x4x8 slice. The times are simulated.
256 devices in a mesh: wide: 32 (over x, y, core), narrow: 8 (over z).
Axes of the slice: x: 4, y: 4, z: 8, core: 2. Of those that a mesh axis runs over, the one named last changes fastest.
Arguments:
- row_vectors: bfloat16 [32768, 2048], P('wide'), may hold values from -0.59765625 to 1.3984375
- col_vectors: bfloat16 [4096, 2048], P('narrow', 'wide'), may hold values from -0.59765625 to 1.3984375
- primal_matrix: bfloat16 [2048, 2048], P('wide'), may hold values from -1 to 3, as said below
- dual_inverse: bfloat16 [2048, 2048], P('wide'), may hold values from -1 to 3, as said below
Outputs:
- factored: float32 [32768, 4096], P('wide', 'narrow')
Inputs may be any that keep to these rules, and one draw needn't show every extreme that they name: `primal_matrix`: symmetric positive definite. `dual_inverse`: symmetric positive definite.
All inputs are finite; a program needn't handle non-finite values.
Results may differ from a plain program's by a relative error of at most 0.0027.
Values may be sent and summed in bfloat16 or wider, within the bound.
A program may use at most 64 MiB of HBM per device.

v0:
```python
import jax
import jax.numpy as jnp
from jax import lax
from jax.sharding import PartitionSpec as P


def from_everyone(x, axis):
    devices = lax.axis_size(axis)
    return lax.all_to_all(jnp.broadcast_to(x[None], (devices, *x.shape)), axis, 0, 0, tiled=True)


def joined_along(tiles, dim):
    shape = list(tiles.shape[1:])
    shape[dim] *= tiles.shape[0]
    return jnp.moveaxis(tiles, 0, dim).reshape(shape)


def gather_directly(x, axis, dim):
    tiles = from_everyone(x, axis)
    return joined_along(tiles, dim)


def broadcast(x, axis, root):
    return lax.dynamic_index_in_dim(lax.all_gather(x, axis), root, 0, keepdims=False)


def in_one_piece(arrays, axis, dim, along):
    both = jnp.concatenate(arrays, axis=along)
    whole, at, finished = (lax.all_gather(both, axis, axis=dim, tiled=True), 0, [])
    for a in arrays:
        finished.append(lax.slice_in_dim(whole, at, at + a.shape[along], axis=along))
        at += a.shape[along]
    return tuple(finished)


def spread(value, axis, source):
    kept = jnp.where(lax.axis_index(axis) == source, value, 0).astype(value.dtype)
    return lax.psum(kept, axis)


def per_device(row_vectors, col_vectors, primal_matrix, dual_inverse):
    wide_count = lax.axis_size("wide")
    wide_index = lax.axis_index("wide")
    narrow_index = lax.axis_index("narrow")
    cone_order = primal_matrix.shape[1]
    panel_width = col_vectors.shape[0]
    panel_share = panel_width // wide_count
    gram_scale = 16.0 / (cone_order * cone_order)
    column_set = gather_directly(col_vectors, "wide", 1)
    local_panel = lax.dynamic_slice_in_dim(column_set, wide_index * panel_share, panel_share, 0)
    panel_set = broadcast(local_panel, "narrow", 0)
    prod_primal = jnp.dot(primal_matrix, column_set.T, preferred_element_type=jnp.float32).astype(
        jnp.bfloat16
    )
    prod_dual = jnp.dot(dual_inverse, column_set.T, preferred_element_type=jnp.float32).astype(
        jnp.bfloat16
    )
    pieces = in_one_piece((prod_primal, prod_dual), "wide", 0, 1)
    row_slice = row_vectors
    panel_slice = panel_set
    gram_primal = jnp.dot(row_slice, pieces[0], preferred_element_type=jnp.float32)
    gram_dual = jnp.dot(row_slice, pieces[1], preferred_element_type=jnp.float32)
    tile_primal = jnp.dot(panel_slice, pieces[0], preferred_element_type=jnp.float32)
    tile_dual = jnp.dot(panel_slice, pieces[1], preferred_element_type=jnp.float32)
    slab = gram_primal * gram_dual * gram_scale
    panel_tile = tile_primal * tile_dual * gram_scale
    gram = gather_directly(panel_tile, "wide", 0)
    panel_primal, panel_dual = (spread(prod_primal, "narrow", 0), spread(prod_dual, "narrow", 0))
    pieces = in_one_piece((panel_primal, panel_dual), "wide", 0, 1)
    row_slice = row_vectors
    panel_slice = panel_set
    first_primal = jnp.dot(row_slice, pieces[0], preferred_element_type=jnp.float32)
    first_dual = jnp.dot(row_slice, pieces[1], preferred_element_type=jnp.float32)
    diag_primal = jnp.dot(panel_slice, pieces[0], preferred_element_type=jnp.float32)
    diag_dual = jnp.dot(panel_slice, pieces[1], preferred_element_type=jnp.float32)
    slab_first = first_primal * first_dual * gram_scale
    diag_share = diag_primal * diag_dual * gram_scale
    diag_block = gather_directly(diag_share, "wide", 0)
    factor = jnp.linalg.cholesky(diag_block)
    panel_cols = jax.scipy.linalg.solve_triangular(factor, slab_first.T, lower=True).T
    solved = jax.scipy.linalg.solve_triangular(factor, gram, lower=True)
    trailing = slab - jnp.dot(panel_cols, solved, precision=lax.Precision.HIGHEST)
    return jnp.where(narrow_index == 0, panel_cols, trailing)


def solution(mesh):
    placed = (P("wide", None), P("narrow", "wide"), P("wide", None), P("wide", None))
    return jax.shard_map(
        per_device, mesh=mesh, in_specs=placed, out_specs=P("wide", "narrow"), check_vma=False
    )
```

profile of v0, /device:TPU:1, one launch (start us, length us, event | category | flops | bytes accessed | tf_op | source)
XLA Modules:
  0.0 366.4 jit_solution(9703437709959540505)
XLA Ops:
  7.4 2.4 broadcast_in_dim.12
  9.8 8.6 %all-to-all-start = ((bf16[32,512,64]{1,2,0:T(8,128)(2,1)}), bf16[32,512,64]{1,2,0:T(8,128)(2,1)S(1)}, u32[]{:S(2)}, u32[]{:S(2)}) async-start(bf16[32,512,64]{1,2,0:T(8,128)(2,1)} %broadcast_in_dim.12), calls=%async_computation | async-start | bytes 4194304 | tf_op jit(solution)/shard_map/all_to_all | solution.py:9
  18.5 28.3 %all-to-all-done = bf16[32,512,64]{1,2,0:T(8,128)(2,1)S(1)} async-done(((bf16[32,512,64]{1,2,0:T(8,128)(2,1)}), bf16[32,512,64]{1,2,0:T(8,128)(2,1)S(1)}, u32[]{:S(2)}, u32[]{:S(2)}) %all-to-all-start) | async-done | bytes 2097184 | tf_op jit(solution)/shard_map/all_to_all | solution.py:9
  46.7 1.1 broadcast_select_fusion
  47.9 1.1 broadcast_select_fusion.1
  49.0 0.7 pad_maximum_fusion.3
  49.8 66.8 %all-reduce.4.cloned.1.call-done = (bf16[64,512]{1,0:T(8,128)(2,1)}, bf16[64,512]{1,0:T(8,128)(2,1)}) async-done(((bf16[64,512]{1,0:T(8,128)(2,1)}, bf16[64,512]{1,0:T(8,128)(2,1)}), (bf16[64,512]{1,0:T(8,128)(2,1)}, bf16[64,512]{1,0:T(8,128)(2,1)})) %all-reduce.4.cloned.1.call-update) | async-done | bytes 131088 | tf_op jit(solution)/shard_map/psum | solution.py:38
  116.6 1.5 pad_maximum_fusion.2
  118.5 19.7 %all-gather = bf16[128,2048]{1,0:T(8,128)(2,1)S(1)} all-gather(bf16[16,2048]{1,0:T(8,128)(2,1)S(1)} %copy.13), channel_id=2, replica_groups=mesh['wide'=32,'narrow'=8] {'narrow'}, dimensions={0}, use_global_device_ids=true | all-gather | bytes 589824 | tf_op jit(solution)/shard_map/all_gather | solution.py:24
  138.2 2.0 fusion.1
  140.2 2.0 fusion.34
  142.2 1.1 broadcast_in_dim.28
  143.3 17.3 %all-to-all-start.2 = ((f32[32,16,512]{2,1,0:T(8,128)}), f32[32,16,512]{2,1,0:T(8,128)S(1)}, u32[]{:S(2)}, u32[]{:S(2)}) async-start(f32[32,16,512]{2,1,0:T(8,128)} %broadcast_in_dim.28), calls=%async_computation.2 | async-start | bytes 2097152 | tf_op jit(solution)/shard_map/all_to_all | solution.py:9
  160.7 6.9 %fusion.3 = f32[512,1024]{1,0:T(8,128)} fusion(bf16[1024,2048]{1,0:T(8,128)(2,1)} %param.4, bf16[2048,1024]{1,0:T(8,128)(2,1)} %all-gather.6.cloned.1.call-done), kind=kOutput, calls=%fused_computation.8 | convolution fusion | flops 2147483648 | bytes 8388608 | tf_op jit(solution)/shard_map/dot_general | solution.py:62
  167.6 3.7 %fusion.7 = f32[512,1024]{1,0:T(8,128)} fusion(bf16[1024,2048]{1,0:T(8,128)(2,1)S(1)} %copy-done.9, bf16[2048,1024]{1,0:T(8,128)(2,1)S(1)} %copy-done.2), kind=kOutput, calls=%fused_computation.12 | convolution fusion | flops 2147483648 | bytes 8388608 | tf_op jit(solution)/shard_map/dot_general | solution.py:61
  171.3 9.7 %all-gather.4.cloned.1.call-done = bf16[2048,1024]{1,0:T(8,128)(2,1)} async-done(((bf16[64,1024]{1,0:T(8,128)(2,1)}), bf16[2048,1024]{1,0:T(8,128)(2,1)}) %all-gather.4.cloned.1.call-update) | async-done | bytes 4194320 | tf_op jit(solution)/shard_map/all_gather | solution.py:29
  181.0 2.0 fusion.11
  183.0 2.0 fusion.37
  185.0 1.1 broadcast_in_dim.14
  186.1 6.4 %all-to-all-start.1 = ((f32[32,16,512]{2,1,0:T(8,128)}), f32[32,16,512]{2,1,0:T(8,128)S(1)}, u32[]{:S(2)}, u32[]{:S(2)}) async-start(f32[32,16,512]{2,1,0:T(8,128)} %broadcast_in_dim.14), calls=%async_computation.1 | async-start | bytes 2097152 | tf_op jit(solution)/shard_map/all_to_all | solution.py:9
  192.5 5.3 %fusion.9 = f32[512,1024]{1,0:T(8,128)S(1)} fusion(bf16[1024,2048]{1,0:T(8,128)(2,1)} %param.4, bf16[2048,1024]{1,0:T(8,128)(2,1)} %all-gather.4.cloned.1.call-done), kind=kOutput, calls=%fused_computation.14 | convolution fusion | flops 2147483648 | bytes 8388608 | tf_op jit(solution)/shard_map/dot_general | solution.py:73
  197.9 3.8 %multiply_multiply_fusion = f32[512,1024]{1,0:T(8,128)} fusion(f32[512,1024]{1,0:T(8,128)S(1)} %fusion.9, bf16[1024,2048]{1,0:T(8,128)(2,1)S(1)} %copy-done.10, bf16[2048,1024]{1,0:T(8,128)(2,1)S(1)} %copy-done.1), kind=kOutput, calls=%fused_computation.5 | convolution fusion | flops 2148532224 | bytes 10485760 | tf_op jit(solution)/shard_map/dot_general | solution.py:72
  201.7 1.0 fusion.95
  202.7 6.3 %all-to-all-done.1 = f32[32,16,512]{2,1,0:T(8,128)S(1)} async-done(((f32[32,16,512]{2,1,0:T(8,128)}), f32[32,16,512]{2,1,0:T(8,128)S(1)}, u32[]{:S(2)}, u32[]{:S(2)}) %all-to-all-start.1) | async-done | bytes 1048608 | tf_op jit(solution)/shard_map/all_to_all | solution.py:9
  209.0 0.3 copy.14
  209.6 11.7 %cholesky.104 = f32[128,128]{1,0:T(8,128)S(1)} custom-call(f32[128,128]{1,0:T(8,128)S(1)} %cholesky.266), custom_call_target="Cholesky" | custom-call | tf_op jit(solution)/shard_map/jit(cholesky)/cholesky | solution.py:79
  221.4 9.8 %custom-call.34 = f32[1,128,128]{1,2,0:T(8,128)S(1)} custom-call(f32[1,128,128]{2,1,0:T(8,128)S(1)} %get-tuple-element.38), custom_call_target="InvertDiagBlocksLowerTriangular" | custom-call | tf_op jit(solution)/shard_map/jit(cholesky)/cholesky | solution.py:79
  231.6 0.5 convolution_subtract_fusion.5
  232.1 11.7 %cholesky.217 = f32[128,128]{1,0:T(8,128)S(1)} custom-call(f32[128,128]{1,0:T(8,128)S(1)} %cholesky.270), custom_call_target="Cholesky" | custom-call | tf_op jit(solution)/shard_map/jit(cholesky)/cholesky | solution.py:79
  243.8 9.8 %custom-call.35 = f32[1,128,128]{1,2,0:T(8,128)S(1)} custom-call(f32[1,128,128]{2,1,0:T(8,128)S(1)} %get-tuple-element.35), custom_call_target="InvertDiagBlocksLowerTriangular" | custom-call | tf_op jit(solution)/shard_map/jit(cholesky)/cholesky | solution.py:79
  253.9 0.4 convolution_subtract_fusion.6
  254.3 11.7 %cholesky.238 = f32[128,128]{1,0:T(8,128)S(1)} custom-call(f32[128,128]{1,0:T(8,128)S(1)} %cholesky.275), custom_call_target="Cholesky" | custom-call | tf_op jit(solution)/shard_map/jit(cholesky)/cholesky | solution.py:79
  266.1 0.7 compare_reduce_fusion.1
  266.8 10.0 %custom-call.36 = f32[1,128,128]{1,2,0:T(8,128)S(1)} custom-call(f32[1,128,128]{2,1,0:T(8,128)S(1)} %get-tuple-element.32), custom_call_target="InvertDiagBlocksLowerTriangular" | custom-call | tf_op jit(solution)/shard_map/jit(cholesky)/cholesky | solution.py:79
  277.0 0.4 convolution_subtract_fusion.7
  277.4 11.7 %cholesky.255 = f32[128,128]{1,0:T(8,128)S(1)} custom-call(f32[128,128]{1,0:T(8,128)S(1)} %convolution_subtract_fusion.7), custom_call_target="Cholesky" | custom-call | tf_op jit(solution)/shard_map/jit(cholesky)/cholesky | solution.py:79
  289.1 0.7 compare_reduce_fusion
  289.9 0.7 compare_reduce_fusion.2
  293.4 10.7 %while.1 = (s32[]{:T(128)}, f32[512,512]{1,0:T(8,128)S(1)}, s32[4,2]{0,1:T(2,128)S(1)}, f32[4,128,128]{2,1,0:T(8,128)}, s32[]{:T(128)}) while((s32[]{:T(128)}, f32[512,512]{1,0:T(8,128)S(1)}, s32[4,2]{0,1:T(2,128)S(1)}, f32[4,128,128]{2,1,0:T(8,128)}, s32[]{:T(128)}) %tuple.32), condition=%wide.while_cond, body=%wide.while_body.sunk | while | flops 2 | bytes 132705 | solution.py:80
  293.4 0.6 fusion.115
  294.0 2.0 bitcast_dynamic-update-slice_fusion.2
  296.1 0.6 fusion.115
  296.7 2.0 bitcast_dynamic-update-slice_fusion.2
  298.8 0.6 fusion.115
  299.4 2.0 bitcast_dynamic-update-slice_fusion.2
  301.5 0.6 fusion.115
  302.1 2.0 bitcast_dynamic-update-slice_fusion.2
  304.1 40.4 %custom-call.37 = f32[4,128,128]{1,2,0:T(8,128)S(1)} custom-call(f32[4,128,128]{2,1,0:T(8,128)} %get-tuple-element.12), custom_call_target="InvertDiagBlocksLowerTriangular" | custom-call | tf_op jit(solution)/shard_map/jit(_solve_triangular)/triangular_solve | solution.py:80
  344.5 0.4 fusion.76
  344.9 0.4 convolution_subtract_fusion.3
  345.3 0.4 fusion.77
  345.8 0.4 convolution_subtract_fusion.2
  346.2 0.4 fusion.79
  346.6 0.6 convolution_subtract_fusion.4
  347.3 0.4 fusion.81
  347.7 0.6 fusion.56
  348.4 0.6 convolution_subtract_fusion.1
  348.9 0.6 fusion.78
  349.6 0.7 convolution_subtract_fusion
  350.3 0.6 fusion.80
  351.0 1.1 fusion.25
  352.1 0.6 fusion.82
  352.7 4.0 %fusion = f32[1024,512]{0,1:T(8,128)S(1)} fusion(f32[512,1024]{1,0:T(8,128)S(1)} %copy-done.12, f32[512,1024]{1,0:T(8,128)S(1)} %copy-done.11, f32[128,1024]{1,0:T(8,128)S(1)} %fusion.82, f32[128,1024]{1,0:T(8,128)S(1)} %fusion.80, f32[128,1024]{1,0:T(8,128)S(1)} %fusion.78, f32[128,1024]{1,0:T(8,128)S(1)} %fusion.56, f32[128,512]{1,0:T(8,128)S(1)} %fusion.81, ...), kind=kOutput, calls=%fused_computation.4 | convolution fusion | flops 3227254784 | bytes 9437185 | tf_op jit(solution)/shard_map/dot_general | solution.py:82
  356.7 1.8 copy.16
  (56 shorter events, 2.4 us)
Async XLA Ops:
  7.4 39.4 %copy-start = (bf16[64,2048]{1,0:T(8,128)(2,1)S(1)}, bf16[64,2048]{1,0:T(8,128)(2,1)}, u32[]{:S(2)}) copy-start(bf16[64,2048]{1,0:T(8,128)(2,1)} %param.7) | copy-start | bytes 786436
  9.8 36.9 %all-to-all-start = ((bf16[32,512,64]{1,2,0:T(8,128)(2,1)}), bf16[32,512,64]{1,2,0:T(8,128)(2,1)S(1)}, u32[]{:S(2)}, u32[]{:S(2)}) async-start(bf16[32,512,64]{1,2,0:T(8,128)(2,1)} %broadcast_in_dim.12), calls=%async_computation | async-start | bytes 4194304 | tf_op jit(solution)/shard_map/all_to_all | solution.py:9
  18.4 29.5 %copy-start.8 = (bf16[64,2048]{1,0:T(8,128)(2,1)S(1)}, bf16[64,2048]{1,0:T(8,128)(2,1)}, u32[]{:S(2)}) copy-start(bf16[64,2048]{1,0:T(8,128)(2,1)} %param.6) | copy-start | bytes 786436
  18.4 98.2 %all-reduce.4.cloned.1.call-start = ((), (), s32[]{:S(2)}) async-start(), calls=%async_computation.5 | async-start | bytes 262144 | tf_op jit(solution)/shard_map/psum | solution.py:38
  49.0 89.3 %all-gather.6.cloned.1.call-start = ((), (), s32[]{:S(2)}) async-start(), calls=%async_computation.4 | async-start | bytes 4325376 | tf_op jit(solution)/shard_map/all_gather | solution.py:29
  49.7 131.3 %all-gather.4.cloned.1.call-start = ((), (), s32[]{:S(2)}) async-start(), calls=%async_computation.3 | async-start | bytes 4325376 | tf_op jit(solution)/shard_map/all_gather | solution.py:29
  143.3 41.7 %all-to-all-start.2 = ((f32[32,16,512]{2,1,0:T(8,128)}), f32[32,16,512]{2,1,0:T(8,128)S(1)}, u32[]{:S(2)}, u32[]{:S(2)}) async-start(f32[32,16,512]{2,1,0:T(8,128)} %broadcast_in_dim.28), calls=%async_computation.2 | async-start | bytes 2097152 | tf_op jit(solution)/shard_map/all_to_all | solution.py:9
  160.7 7.0 %copy-start.2 = (bf16[2048,1024]{1,0:T(8,128)(2,1)S(1)}, bf16[2048,1024]{1,0:T(8,128)(2,1)}, u32[]{:S(2)}) copy-start(bf16[2048,1024]{1,0:T(8,128)(2,1)} %all-gather.6.cloned.1.call-done) | copy-start | bytes 12582916
  160.7 7.0 %copy-start.9 = (bf16[1024,2048]{1,0:T(8,128)(2,1)S(1)}, bf16[1024,2048]{1,0:T(8,128)(2,1)}, u32[]{:S(2)}) copy-start(bf16[1024,2048]{1,0:T(8,128)(2,1)} %param.4) | copy-start | bytes 12582916
  186.1 22.9 %all-to-all-start.1 = ((f32[32,16,512]{2,1,0:T(8,128)}), f32[32,16,512]{2,1,0:T(8,128)S(1)}, u32[]{:S(2)}, u32[]{:S(2)}) async-start(f32[32,16,512]{2,1,0:T(8,128)} %broadcast_in_dim.14), calls=%async_computation.1 | async-start | bytes 2097152 | tf_op jit(solution)/shard_map/all_to_all | solution.py:9
  192.5 5.4 %copy-start.1 = (bf16[2048,1024]{1,0:T(8,128)(2,1)S(1)}, bf16[2048,1024]{1,0:T(8,128)(2,1)}, u32[]{:S(2)}) copy-start(bf16[2048,1024]{1,0:T(8,128)(2,1)} %all-gather.4.cloned.1.call-done) | copy-start | bytes 12582916
  192.5 5.4 %copy-start.10 = (bf16[1024,2048]{1,0:T(8,128)(2,1)S(1)}, bf16[1024,2048]{1,0:T(8,128)(2,1)}, u32[]{:S(2)}) copy-start(bf16[1024,2048]{1,0:T(8,128)(2,1)} %param.4) | copy-start | bytes 12582916
  254.3 90.2 %copy-start.5 = (f32[8,16,512]{2,1,0:T(8,128)S(1)}, f32[8,16,512]{2,1,0:T(8,128)}, u32[]{:S(2)}) copy-start(f32[8,16,512]{2,1,0:T(8,128)} %get-tuple-element.25) | copy-start | bytes 786436
  276.8 68.2 %copy-start.4 = (f32[8,16,512]{2,1,0:T(8,128)S(1)}, f32[8,16,512]{2,1,0:T(8,128)}, u32[]{:S(2)}) copy-start(f32[8,16,512]{2,1,0:T(8,128)} %get-tuple-element.28) | copy-start | bytes 786436
  293.2 52.6 %copy-start.7 = (f32[8,16,512]{2,1,0:T(8,128)S(1)}, f32[8,16,512]{2,1,0:T(8,128)}, u32[]{:S(2)}) copy-start(f32[8,16,512]{2,1,0:T(8,128)} %get-tuple-element.27) | copy-start | bytes 786436
  304.1 42.6 %copy-start.6 = (f32[8,16,512]{2,1,0:T(8,128)S(1)}, f32[8,16,512]{2,1,0:T(8,128)}, u32[]{:S(2)}) copy-start(f32[8,16,512]{2,1,0:T(8,128)} %get-tuple-element.26) | copy-start | bytes 786436
  345.3 2.4 copy-start.3
  350.3 2.4 copy-start.12
  351.0 1.8 copy-start.11
Sparse Core Ops, SparseCore 0:
  49.1 67.4 all-reduce.3
Sparse Core Ops, SparseCore 1:
  52.0 50.4 all-gather.5
  118.2 62.8 all-gather.3
where the time goes:
time: 373 us; the launch traced here: 366 us
  other arithmetic  122 us (33%)
  waiting for transfers between devices  111 us (30%)
  matrix products  43.9 us (12%)
  starting transfers between devices  32.5 us (9%)
  blocking collectives  19.7 us (5%)
  local copies, waits for them, and re-layouts  19.1 us (5%)
  between operations  18.4 us (5%)
    another operation x14, other arithmetic, per_device(): factor = jnp.linalg.cholesky(diag_block)  78.7 us
    psum x1, waiting for transfers between devices, spread(): return lax.psum(kept, axis)  66.8 us
    another operation x3, other arithmetic, per_device(): jax.scipy.linalg.solve_triangular(factor, slab_first.T, lower=True)  40.5 us
    all_to_all x3, waiting for transfers between devices, from_everyone(): lax.all_to_all(jnp.broadcast_to(x[None], (devices, *x.shape)), axis, 0, 0...  34.6 us
    all_to_all x3, starting transfers between devices, from_everyone(): lax.all_to_all(jnp.broadcast_to(x[None], (devices, *x.shape)), axis, 0, 0...  32.3 us
    all_gather x1, blocking collectives, broadcast(): lax.all_gather(x, axis)  19.7 us
    dot_general x2, matrix products, per_device(): jnp.dot(row_slice, pieces[1], preferred_element_type=jnp.float32)  12.3 us
    another operation x12, local copies, waits for them, and re-layouts  10.7 us
  transfers between devices with their start and end apart: 6, of which 4 were waited for; matrix products, arithmetic and copies ran while one was open for 9% of the time, Pallas kernels for 0%

commit v1 on v0

v1 whole, which is shorter than its diff:
```python
import jax
import jax.numpy as jnp
from jax import lax
from jax.experimental import pallas as pl
from jax.experimental.pallas import tpu as pltpu
from jax.sharding import PartitionSpec as P

F32 = jnp.float32
BF16 = jnp.bfloat16
HIGHEST = lax.Precision.HIGHEST
MESH = pl.DeviceIdType.MESH
SIDE = 4
TILE = 128


def lane_copy(x, k):
    return jnp.take_along_axis(x, jnp.full(x.shape, k, jnp.int32), axis=1)


def row_copy(x, r):
    return jnp.broadcast_to(x[r : r + 1, :], x.shape)


def split(x):
    hi = x.astype(BF16)
    return hi, (x - hi.astype(F32)).astype(BF16)


def dot(a, b):
    return jnp.dot(a, b, preferred_element_type=F32)


def dot_first(a, b):
    return lax.dot_general(a, b, (((0,), (0,)), ((), ())), preferred_element_type=F32)


def factor_tile(tile):
    groups = TILE // 8
    lanes = lax.broadcasted_iota(jnp.int32, (8, TILE), 1)
    rows = lax.broadcasted_iota(jnp.int32, (8, TILE), 0)
    left = [tile[8 * g : 8 * g + 8, :] for g in range(groups)]
    right = [(lanes == rows + 8 * g).astype(F32) for g in range(groups)]
    for s in range(groups):
        cols = {g: [lane_copy(left[g], 8 * s + j) for j in range(8)] for g in range(s, groups)}
        scale = jnp.zeros((8, TILE), F32)
        for j in range(8):
            pivot = row_copy(cols[s][j], j)
            inv = 1.0 / pivot
            lead_left, lead_right = row_copy(left[s], j), row_copy(right[s], j)
            lead_cols = [row_copy(cols[s][k], j) for k in range(j + 1, 8)]
            scale = jnp.where(rows == j, pivot, scale)
            for g in range(s, groups):
                mult = cols[g][j] * inv
                if g == s:
                    mult = jnp.where(rows > j, mult, 0.0)
                left[g] = left[g] - mult * lead_left
                right[g] = right[g] - mult * lead_right
                for k in range(j + 1, 8):
                    cols[g][k] = cols[g][k] - mult * lead_cols[k - j - 1]
        tile[8 * s : 8 * s + 8, :] = right[s] * lax.rsqrt(scale)


def factor_block(aug, tile, b):
    size = aug.shape[0]
    at = pl.ds(pl.multiple_of(b * TILE, TILE), TILE)
    tile[...] = aug[at, at]
    factor_tile(tile)
    rows = lax.broadcasted_iota(jnp.int32, (TILE, TILE), 0)
    lanes = lax.broadcasted_iota(jnp.int32, (TILE, TILE), 1)
    aug[at, at] = (rows == lanes).astype(F32)
    aug[at, :] = jnp.dot(tile[...], aug[at, :], precision=HIGHEST, preferred_element_type=F32)

    def below(i, _):
        to = pl.ds(pl.multiple_of(i * TILE, TILE), TILE)
        coef = aug[at, to]
        aug[to, at] = jnp.zeros((TILE, TILE), F32)
        aug[to, :] = aug[to, :] - lax.dot_general(
            coef, aug[at, :], (((0,), (0,)), ((), ())), precision=HIGHEST, preferred_element_type=F32
        )
        return 0

    lax.fori_loop(b + 1, size // TILE, below, 0)


class Gather:
    def __init__(self, view, share, sems):
        self.view, self.share, self.sems = view, share, sems
        wide, self.narrow = lax.axis_index("wide"), lax.axis_index("narrow")
        self.core = lax.rem(wide, 2)
        x, y = wide // 8, lax.rem(wide // 2, SIDE)
        self.step_p, self.step_q = 2 + 6 * self.core, 8 - 6 * self.core
        self.p = y + self.core * (x - y)
        self.q = x + self.core * (y - x)
        self.partner = wide + 1 - 2 * self.core

    def around(self, value, by):
        return lax.rem(value + by, SIDE)

    def wide(self, dp, dq):
        p, q = self.around(self.p, dp), self.around(self.q, dq)
        return p * self.step_p + q * self.step_q + self.core

    def rows(self, dp, dq, half=None):
        start, count = self.wide(dp, dq) * self.share, self.share
        if half is not None:
            count = self.share // 2
            start = start + half * count
        return self.view(pl.ds(pl.multiple_of(start, count), count))

    def send(self, ref, to, sem):
        pltpu.make_async_remote_copy(
            src_ref=ref, dst_ref=ref, send_sem=self.sems.at[16], recv_sem=self.sems.at[sem],
            device_id=(to, self.narrow), device_id_type=MESH,
        ).start()

    def got(self, ref, sem):
        pltpu.make_async_remote_copy(
            src_ref=ref, dst_ref=ref, send_sem=self.sems.at[16], recv_sem=self.sems.at[sem],
            device_id=(self.partner, self.narrow), device_id_type=MESH,
        ).wait_recv()

    def second(self, dp, k):
        ref = self.rows(dp, 0)
        self.send(ref, self.wide(0, 1), 3 + k)
        self.send(ref, self.wide(0, 3), 7 + k)
        self.send(ref, self.partner, 15)

    def own(self):
        ref = self.rows(0, 0)
        self.send(ref, self.wide(1, 0), 0)
        self.send(ref, self.wide(3, 0), 1)
        self.second(0, 0)

    def first_near(self):
        for side, (dp, to) in enumerate(((3, 1), (1, 3))):
            self.got(self.rows(dp, 0), side)
            self.send(self.rows(dp, 0, side), self.wide(to, 0), 2)
            self.second(dp, 1 + side)

    def first_far(self):
        self.got(self.rows(2, 0), 2)
        self.second(2, 3)

    def second_near(self, ks=(0, 1, 2, 3)):
        for k in ks:
            dp = (0, 3, 1, 2)[k]
            for side, (dq, to) in enumerate(((3, 1), (1, 3))):
                self.got(self.rows(dp, dq), 3 + 4 * side + k)
                self.send(self.rows(dp, dq, side), self.wide(0, to), 11 + k)
                self.send(self.rows(dp, dq), self.partner, 15)

    def second_far(self):
        for k, dp in enumerate((0, 3, 1, 2)):
            self.got(self.rows(dp, 2), 11 + k)
            self.send(self.rows(dp, 2), self.partner, 15)

    def last(self):
        self.got(self.view(pl.ds(0, 16 * self.share)), 15)

    def sent(self):
        ref = self.view(pl.ds(0, 31 * self.share))
        pltpu.make_async_remote_copy(
            src_ref=ref, dst_ref=ref, send_sem=self.sems.at[16], recv_sem=self.sems.at[15],
            device_id=(self.partner, self.narrow), device_id_type=MESH,
        ).wait_send()


def kernel(
    row_ref, col_ref, primal_ref, dual_ref, out_ref,
    rows_v, both_v, cols_v, prods_v, panel_v, aug, tile, gram_v,
    first_hi, first_lo, slab_v, inv_hi, inv_lo, mid_hi, mid_lo, mix_hi, mix_lo,
    sems, z_sems, in_sems, out_sems,
):
    wide, narrow = lax.axis_index("wide"), lax.axis_index("narrow")
    planes = lax.axis_size("narrow")
    order = rows_v.shape[1]
    panel = gram_v.shape[0]
    share = both_v.shape[0] // 2
    scale = 16.0 / (order * order)

    load_rows = pltpu.make_async_copy(row_ref, rows_v, in_sems.at[0])
    load_primal = pltpu.make_async_copy(primal_ref, both_v.at[pl.ds(0, share)], in_sems.at[1])
    load_dual = pltpu.make_async_copy(dual_ref, both_v.at[pl.ds(share, share)], in_sems.at[2])
    load_primal.start()
    load_dual.start()
    load_rows.start()

    mine = pl.ds(pl.multiple_of(wide * share, share), share)
    shard = col_ref[...].T
    cols_v[1, mine, :] = shard

    @pl.when(narrow == 0)
    def _():
        cols_v[0, mine, :] = shard

    panel_cols = Gather(lambda r: cols_v.at[0, r], share, sems.at[0])
    block_cols = Gather(lambda r: cols_v.at[1, r], share, sems.at[1])
    panel_prods = Gather(lambda r: prods_v.at[0, :, r], share, sems.at[2])
    block_prods = Gather(lambda r: prods_v.at[1, :, r], share, sems.at[3])

    barrier = pltpu.get_barrier_semaphore()
    g = panel_cols
    for to in (g.wide(1, 0), g.wide(3, 0), g.wide(0, 1), g.wide(0, 3), g.partner):
        pl.semaphore_signal(barrier, inc=1, device_id=(to, narrow), device_id_type=MESH)

    @pl.when(narrow == 0)
    def _():
        for z in range(1, planes):
            pl.semaphore_signal(barrier, inc=1, device_id=(wide, z), device_id_type=MESH)
        pl.semaphore_wait(barrier, 5 + planes - 1)

    @pl.when(narrow != 0)
    def _():
        pl.semaphore_signal(barrier, inc=1, device_id=(wide, 0), device_id_type=MESH)
        pl.semaphore_wait(barrier, 6)

    def z_copy(z):
        ref = cols_v.at[0, mine]
        return pltpu.make_async_remote_copy(
            src_ref=ref, dst_ref=ref, send_sem=z_sems.at[0], recv_sem=z_sems.at[1],
            device_id=(wide, z), device_id_type=MESH,
        )

    @pl.when(narrow == 0)
    def _():
        for z in (4, 3, 5, 2, 6, 1, 7):
            z_copy(z).start()

    block_cols.own()
    block_cols.first_near()

    @pl.when(narrow != 0)
    def _():
        z_copy(0).wait_recv()

    panel_cols.own()
    block_cols.first_far()
    panel_cols.first_near()
    block_cols.second_near()
    panel_cols.first_far()
    block_cols.second_far()
    panel_cols.second_near()
    panel_cols.second_far()

    def products(which):
        done = dot(both_v[...], cols_v[which]).astype(BF16)
        prods_v[which, 0, mine, :] = done[:share]
        prods_v[which, 1, mine, :] = done[share:]

    load_primal.wait()
    load_dual.wait()
    panel_cols.last()
    products(0)
    panel_prods.own()
    block_cols.last()
    products(1)
    panel_prods.first_near()
    block_prods.own()

    def turn(t, _):
        at = pl.ds(pl.multiple_of(t * TILE, TILE), TILE)
        panel_v[:, at] = cols_v[0, at, :].T
        return 0

    lax.fori_loop(0, order // TILE, turn, 0)

    panel_prods.first_far()
    block_prods.first_near()
    panel_prods.second_near()
    block_prods.first_far()
    panel_prods.second_far()
    panel_prods.last()

    def hadamard(lhs, which):
        return dot(lhs, prods_v[which, 0]) * dot(lhs, prods_v[which, 1]) * scale

    step = 256

    def each(count, body):
        def one(t, _):
            body(pl.ds(pl.multiple_of(t * step, step), step))
            return 0

        lax.fori_loop(0, count // step, one, 0)

    @lambda body: each(panel, body)
    def _(at):
        aug[at, :] = hadamard(panel_v[at, :], 0)

    def chol(b, _):
        factor_block(aug, tile, b)

        @pl.when(b == 0)
        def _():
            block_prods.second_near()

        @pl.when(b == 1)
        def _():
            block_prods.second_far()

        return 0

    lax.fori_loop(0, panel // TILE, chol, 0)

    load_rows.wait()

    @lambda body: each(rows_v.shape[0], body)
    def _(at):
        first_hi[at, :], first_lo[at, :] = split(hadamard(rows_v[at, :], 0))

    block_prods.last()

    @lambda body: each(panel, body)
    def _(at):
        gram_v[at, :] = hadamard(panel_v[at, :], 1)

    @lambda body: each(rows_v.shape[0], body)
    def _(at):
        slab_v[at, :] = hadamard(rows_v[at, :], 1)

    for b in range(panel // TILE):
        at = pl.ds(b * TILE, TILE)
        lanes = lax.broadcasted_iota(jnp.int32, (TILE, panel), 1)
        kept = jnp.where(lanes < (b + 1) * TILE, aug[at, :], 0.0)
        inv_hi[at, :], inv_lo[at, :] = split(kept)
        gram_hi, gram_lo = split(gram_v[at, :])
        mix_hi[at, :], mix_lo[at, :] = gram_hi, gram_lo

    @lambda body: each(panel, body)
    def _(at):
        solved = dot(inv_hi[at, :], mix_hi[...]) + (
            dot(inv_hi[at, :], mix_lo[...]) + dot(inv_lo[at, :], mix_hi[...])
        )
        rows = lax.broadcasted_iota(jnp.int32, (step, panel), 0) + at.start
        lanes = lax.broadcasted_iota(jnp.int32, (step, panel), 1)
        solved = jnp.where(narrow == 0, jnp.where(rows == lanes, -1.0, 0.0), solved)
        mid_hi[at, :], mid_lo[at, :] = split(solved)

    @lambda body: each(panel, body)
    def _(at):
        mixed = dot_first(inv_hi[:, at], mid_hi[...]) + (
            dot_first(inv_hi[:, at], mid_lo[...]) + dot_first(inv_lo[:, at], mid_hi[...])
        )
        mix_hi[at, :], mix_lo[at, :] = split(mixed)

    @lambda body: each(rows_v.shape[0], body)
    def _(at):
        taken = dot(first_hi[at, :], mix_hi[...]) + (
            dot(first_hi[at, :], mix_lo[...]) + dot(first_lo[at, :], mix_hi[...])
        )
        slab_v[at, :] = jnp.where(narrow == 0, 0.0, slab_v[at, :]) - taken

    store = pltpu.make_async_copy(slab_v, out_ref, out_sems.at[0])
    store.start()
    store.wait()

    for g in (block_cols, panel_cols, panel_prods, block_prods):
        g.sent()

    @pl.when(narrow == 0)
    def _():
        ref = cols_v.at[0, pl.ds(0, (planes - 1) * share)]
        pltpu.make_async_remote_copy(
            src_ref=ref, dst_ref=ref, send_sem=z_sems.at[0], recv_sem=z_sems.at[1],
            device_id=(wide, 1), device_id_type=MESH,
        ).wait_send()


def per_device(row_vectors, col_vectors, primal_matrix, dual_inverse):
    rows, order = row_vectors.shape
    panel = col_vectors.shape[0]
    share = primal_matrix.shape[0]
    whole = pl.BlockSpec(memory_space=pl.ANY)
    small, square = (panel, order), (panel, panel)
    return pl.pallas_call(
        kernel,
        out_shape=jax.ShapeDtypeStruct((rows, panel), F32),
        in_specs=[whole, pl.BlockSpec(memory_space=pltpu.VMEM), whole, whole],
        out_specs=whole,
        scratch_shapes=[
            pltpu.VMEM((rows, order), BF16),
            pltpu.VMEM((2 * share, order), BF16),
            pltpu.VMEM((2, order, panel), BF16),
            pltpu.VMEM((2, 2, order, panel), BF16),
            pltpu.VMEM(small, BF16),
            pltpu.VMEM(square, F32),
            pltpu.VMEM((TILE, TILE), F32),
            pltpu.VMEM(square, F32),
            pltpu.VMEM((rows, panel), BF16),
            pltpu.VMEM((rows, panel), BF16),
            pltpu.VMEM((rows, panel), F32),
            *[pltpu.VMEM(square, BF16)] * 6,
            pltpu.SemaphoreType.DMA((4, 17)),
            pltpu.SemaphoreType.DMA((2,)),
            pltpu.SemaphoreType.DMA((3,)),
            pltpu.SemaphoreType.DMA((1,)),
        ],
        compiler_params=pltpu.CompilerParams(
            collective_id=0, has_side_effects=True, vmem_limit_bytes=58 << 20
        ),
    )(row_vectors, col_vectors, primal_matrix, dual_inverse)


def solution(mesh):
    placed = (P("wide", None), P("narrow", "wide"), P("wide", None), P("wide", None))
    return jax.shard_map(
        per_device, mesh=mesh, in_specs=placed, out_specs=P("wide", "narrow"), check_vma=False
    )
```

time: 373 us -> 101 us (0.27)
  the two profiles are of different devices: /device:TPU:1 before, /device:TPU:32 now
where the time goes in v1:
time: 101 us
  Pallas kernels  96.6 us (96%)
  local copies, waits for them, and re-layouts  4.68 us (5%)
    pallas_call x1, Pallas kernels, per_device(): pl.pallas_call(kernel, out_shape=jax.ShapeDtypeStruct((rows, panel), F32)...  96.6 us
    unnamed x2, local copies, waits for them, and re-layouts  4.68 us

profile of v1, /device:TPU:32, one launch (start us, length us, event | category | flops | bytes accessed | tf_op | source)
XLA Modules:
  0.0 101.3 jit_solution(9199174054760696509)
XLA Ops:
  0.0 1.6 %copy.5.col_ref = bf16[512,64]{1,0:T(8,128)(2,1)} copy(bf16[512,64]{0,1:T(8,128)(2,1)} %param.5) | data formatting | bytes 131072 | tf_op args[1]
  1.6 96.6 %shard_map.46 = f32[1024,512]{1,0:T(8,128)} custom-call(bf16[1024,2048]{1,0:T(8,128)(2,1)} %row_ref.1, bf16[512,64]{1,0:T(8,128)(2,1)} %copy.5.col_ref, bf16[64,2048]{1,0:T(8,128)(2,1)} %primal_ref.1, bf16[64,2048]{1,0:T(8,128)(2,1)} %dual_ref.1), custom_call_target="tpu_custom_call" | custom-call | tf_op jit(solution)/shard_map/pallas_call | solution.py:375
  98.2 3.1 %copy.7 = f32[1024,512]{1,0:T(8,128)} copy(f32[1024,512]{1,0:T(8,128)} %shard_map.46) | data formatting | bytes 4194304

commit v2 on v1

--- a/solution.py
+++ b/solution.py
@@ -60,10 +60,11 @@
         tile[8 * s : 8 * s + 8, :] = right[s] * lax.rsqrt(scale)
 
 
-def factor_block(aug, tile, b):
+def factor_block(aug, tile, b, beside):
     size = aug.shape[0]
     at = pl.ds(pl.multiple_of(b * TILE, TILE), TILE)
     tile[...] = aug[at, at]
+    beside()
     factor_tile(tile)
     rows = lax.broadcasted_iota(jnp.int32, (TILE, TILE), 0)
     lanes = lax.broadcasted_iota(jnp.int32, (TILE, TILE), 1)
@@ -167,14 +168,14 @@
 
 def kernel(
     row_ref, col_ref, primal_ref, dual_ref, out_ref,
-    rows_v, both_v, cols_v, prods_v, panel_v, aug, tile, gram_v,
+    rows_v, both_v, cols_v, prods_v, panel_v, aug, tile,
     first_hi, first_lo, slab_v, inv_hi, inv_lo, mid_hi, mid_lo, mix_hi, mix_lo,
-    sems, z_sems, in_sems, out_sems,
+    sems, z_sems, in_sems,
 ):
     wide, narrow = lax.axis_index("wide"), lax.axis_index("narrow")
     planes = lax.axis_size("narrow")
     order = rows_v.shape[1]
-    panel = gram_v.shape[0]
+    panel = aug.shape[0]
     share = both_v.shape[0] // 2
     scale = 16.0 / (order * order)
 
@@ -186,7 +187,7 @@
     load_rows.start()
 
     mine = pl.ds(pl.multiple_of(wide * share, share), share)
-    shard = col_ref[...].T
+    shard = col_ref[...]
     cols_v[1, mine, :] = shard
 
     @pl.when(narrow == 0)
@@ -287,44 +288,43 @@
     def _(at):
         aug[at, :] = hadamard(panel_v[at, :], 0)
 
-    def chol(b, _):
-        factor_block(aug, tile, b)
+    half = rows_v.shape[0] // 2
+    blocks = panel // TILE
+
+    def early(b, _):
+        def beside():
+            at = pl.ds(pl.multiple_of(b * half, half), half)
+            first_hi[at, :], first_lo[at, :] = split(hadamard(rows_v[at, :], 0))
+
+        factor_block(aug, tile, b, beside)
 
         @pl.when(b == 0)
         def _():
             block_prods.second_near()
 
-        @pl.when(b == 1)
-        def _():
-            block_prods.second_far()
-
         return 0
 
-    lax.fori_loop(0, panel // TILE, chol, 0)
+    def late(b, _):
+        def beside():
+            at = pl.ds(pl.multiple_of((b - blocks // 2) * half, half), half)
+            slab_v[at, :] = hadamard(rows_v[at, :], 1)
+            at = pl.ds(pl.multiple_of((b - blocks // 2) * (panel // 2), panel // 2), panel // 2)
+            mix_hi[at, :], mix_lo[at, :] = split(hadamard(panel_v[at, :], 1))
+
+        factor_block(aug, tile, b, beside)
+        return 0
 
     load_rows.wait()
-
-    @lambda body: each(rows_v.shape[0], body)
-    def _(at):
-        first_hi[at, :], first_lo[at, :] = split(hadamard(rows_v[at, :], 0))
-
+    lax.fori_loop(0, blocks // 2, early, 0)
+    block_prods.second_far()
     block_prods.last()
-
-    @lambda body: each(panel, body)
-    def _(at):
-        gram_v[at, :] = hadamard(panel_v[at, :], 1)
-
-    @lambda body: each(rows_v.shape[0], body)
-    def _(at):
-        slab_v[at, :] = hadamard(rows_v[at, :], 1)
+    lax.fori_loop(blocks // 2, blocks, late, 0)
 
     for b in range(panel // TILE):
         at = pl.ds(b * TILE, TILE)
         lanes = lax.broadcasted_iota(jnp.int32, (TILE, panel), 1)
         kept = jnp.where(lanes < (b + 1) * TILE, aug[at, :], 0.0)
         inv_hi[at, :], inv_lo[at, :] = split(kept)
-        gram_hi, gram_lo = split(gram_v[at, :])
-        mix_hi[at, :], mix_lo[at, :] = gram_hi, gram_lo
 
     @lambda body: each(panel, body)
     def _(at):
@@ -348,11 +348,8 @@
         taken = dot(first_hi[at, :], mix_hi[...]) + (
             dot(first_hi[at, :], mix_lo[...]) + dot(first_lo[at, :], mix_hi[...])
         )
-        slab_v[at, :] = jnp.where(narrow == 0, 0.0, slab_v[at, :]) - taken
-
-    store = pltpu.make_async_copy(slab_v, out_ref, out_sems.at[0])
-    store.start()
-    store.wait()
+        out_ref[at, :] = jnp.where(narrow == 0, 0.0, slab_v[at, :]) - taken
+
 
     for g in (block_cols, panel_cols, panel_prods, block_prods):
         g.sent()
@@ -370,13 +367,13 @@
     rows, order = row_vectors.shape
     panel = col_vectors.shape[0]
     share = primal_matrix.shape[0]
-    whole = pl.BlockSpec(memory_space=pl.ANY)
+    whole = pl.BlockSpec(memory_space=pltpu.HBM)
     small, square = (panel, order), (panel, panel)
     return pl.pallas_call(
         kernel,
         out_shape=jax.ShapeDtypeStruct((rows, panel), F32),
         in_specs=[whole, pl.BlockSpec(memory_space=pltpu.VMEM), whole, whole],
-        out_specs=whole,
+        out_specs=pl.BlockSpec(memory_space=pltpu.VMEM),
         scratch_shapes=[
             pltpu.VMEM((rows, order), BF16),
             pltpu.VMEM((2 * share, order), BF16),
@@ -385,7 +382,6 @@
             pltpu.VMEM(small, BF16),
             pltpu.VMEM(square, F32),
             pltpu.VMEM((TILE, TILE), F32),
-            pltpu.VMEM(square, F32),
             pltpu.VMEM((rows, panel), BF16),
             pltpu.VMEM((rows, panel), BF16),
             pltpu.VMEM((rows, panel), F32),
@@ -393,12 +389,11 @@
             pltpu.SemaphoreType.DMA((4, 17)),
             pltpu.SemaphoreType.DMA((2,)),
             pltpu.SemaphoreType.DMA((3,)),
-            pltpu.SemaphoreType.DMA((1,)),
         ],
         compiler_params=pltpu.CompilerParams(
-            collective_id=0, has_side_effects=True, vmem_limit_bytes=58 << 20
+            collective_id=0, has_side_effects=True, vmem_limit_bytes=61 << 20
         ),
-    )(row_vectors, col_vectors, primal_matrix, dual_inverse)
+    )(row_vectors, col_vectors.T, primal_matrix, dual_inverse)
 
 
 def solution(mesh):

time: 101 us -> 90.2 us (0.89)
  Pallas kernels: 96.6 us -> 86.7 us
  local copies, waits for them, and re-layouts: 4.68 us -> 3.08 us
    pallas_call x1, Pallas kernels: 96.6 us -> 86.7 us  [per_device(): pl.pallas_call(kernel, out_shape=jax.ShapeDtypeStruct((rows, panel), F32)...]
    unnamed x2 -> x1, local copies, waits for them, and re-layouts: 4.68 us -> 3.08 us
where the time goes in v2:
time: 90.2 us; the launch traced here: 89.8 us
  Pallas kernels  86.7 us (96%)
  local copies, waits for them, and re-layouts  3.08 us (3%)
    pallas_call x1, Pallas kernels, per_device(): pl.pallas_call(kernel, out_shape=jax.ShapeDtypeStruct((rows, panel), F32)...  86.7 us
    unnamed x1, local copies, waits for them, and re-layouts  3.08 us

profile of v2, /device:TPU:32, one launch (start us, length us, event | category | flops | bytes accessed | tf_op | source)
XLA Modules:
  0.0 89.8 jit_solution(8519042808108100327)
XLA Ops:
  0.0 86.7 %shard_map.46 = f32[1024,512]{1,0:T(8,128)} custom-call(bf16[1024,2048]{1,0:T(8,128)(2,1)} %row_ref.1, bf16[64,512]{1,0:T(8,128)(2,1)} %bitcast.1, bf16[64,2048]{1,0:T(8,128)(2,1)} %primal_ref.1, bf16[64,2048]{1,0:T(8,128)(2,1)} %dual_ref.1), custom_call_target="tpu_custom_call" | custom-call | tf_op jit(solution)/shard_map/pallas_call | solution.py:372
  86.8 3.1 %copy.6 = f32[1024,512]{1,0:T(8,128)} copy(f32[1024,512]{1,0:T(8,128)} %shard_map.46) | data formatting | bytes 4194304
